TPU v7x, 32 devices: a whole 2x2x4 slice. The times are simulated.
32 devices in a mesh: gx: 8 (over z, x), gy: 4 (over y, core).
Axes of the slice: x: 2, y: 2, z: 4, core: 2. Of those that a mesh axis runs over, the one named last changes fastest.
Arguments:
- pooled: bfloat16 [4096, 8, 128], P(('gx', 'gy')), may hold values from -6 to 6
- cotangent: bfloat16 [4096, 28, 128], P(('gx', 'gy')), may hold values from -0.09375 to 0.09375
- bilinear: bfloat16 [7, 128, 128], replicated, may hold values from -0.5 to 0.5
- bag_ids: int32 [4096, 8, 4], P(('gx', 'gy')), may hold values from 0 to 8191, as said below
- bag_lens: int32 [4096, 8], P(('gx', 'gy')), may hold values from 1 to 4
- row_home: int32 [8, 8192], replicated, may hold values from 0 to 8191, as said below
Outputs:
- weight_grad: float32 [7, 128, 128], replicated
- table_grad: float32 [8192, 8, 128], P(('gx', 'gy'))
Inputs may be any that keep to these rules, and one draw needn't show every extreme that they name: Each row row_home[f] is a permutation; row r of field f's table is stored at position row_home[f, r] of table_grad's first dimension. Only the first bag_lens entries of a bag are live. The stored position q = row_home[f, bag_ids[sample, f, k]] of an entry lies in the block of 256 positions of device q // 256 (devices in gx+gy order); among all entries of one device's samples, live or not, at most 256 lie in any one device's block; in every device's entries some block is hit exactly 256 times, and one block is hit exactly 256 times by the entries of every device.
All inputs are finite; a program needn't handle non-finite values.
Results may differ from a plain program's by a relative error of at most 0.0035.
Values may be sent and summed in bfloat16 or wider, within the bound.
No kernel may reach another device: no remote copies, remote signals or barrier semaphores. Data moves between devices by JAX's collectives and lax.ppermute only.
A program may use at most 64 MiB of HBM per device.

v0:
```python
import jax
import jax.numpy as jnp
from jax import lax
from jax.sharding import PartitionSpec as P

FIELDS = 8
BAG = 4
R_DEV = 256


def pair_list(fields):
    return [(i, j) for i in range(fields) for j in range(i + 1, fields)]


def on_device(pooled, cotangent, bilinear, bag_ids, bag_lens, row_home):
    pair_order = pair_list(FIELDS)
    samples = pooled.shape[0]
    width = pooled.shape[2]
    projected = jnp.einsum(
        "bfd,fde->bfe", pooled[:, : FIELDS - 1], bilinear, preferred_element_type=jnp.float32
    )
    upper_terms = []
    for i in range(FIELDS - 1):
        running = jnp.zeros((samples, width), jnp.float32)
        for p, (a, c) in enumerate(pair_order):
            if a == i:
                running = running + cotangent[:, p].astype(jnp.float32) * pooled[:, c].astype(
                    jnp.float32
                )
        upper_terms.append(running)
    upper_bf = jnp.stack(upper_terms, 1).astype(jnp.bfloat16)
    local_weight = jnp.einsum(
        "bfd,bfe->fde", pooled[:, : FIELDS - 1], upper_bf, preferred_element_type=jnp.float32
    )
    weight_grad = lax.psum(local_weight, ("gx", "gy"))
    back_terms = jnp.einsum("bfe,fde->bfd", upper_bf, bilinear, preferred_element_type=jnp.float32)
    field_list = []
    for i in range(FIELDS):
        running = back_terms[:, i] if i < FIELDS - 1 else jnp.zeros((samples, width), jnp.float32)
        for p, (a, c) in enumerate(pair_order):
            if c == i:
                running = running + cotangent[:, p].astype(jnp.float32) * projected[:, a]
        field_list.append(running)
    field_grads = jnp.stack(field_list, 1).astype(jnp.bfloat16)
    size_gx = lax.axis_size("gx")
    size_gy = lax.axis_size("gy")
    owners_all = size_gx * size_gy
    entries = samples * FIELDS * BAG
    capacity = max(1, 2 * entries // owners_all)
    sentinel = R_DEV * FIELDS
    field_index = jnp.arange(FIELDS, dtype=jnp.int32)[None, :, None]
    stored = row_home[field_index, bag_ids]
    live = jnp.arange(BAG, dtype=jnp.int32)[None, None, :] < bag_lens[:, :, None]
    owner = (stored // R_DEV).reshape(-1)
    target = jnp.where(live, stored % R_DEV * FIELDS + field_index, sentinel).reshape(-1)
    values = jnp.where(live[:, :, :, None], field_grads[:, :, None, :], jnp.zeros((), jnp.bfloat16))
    values = values.reshape(entries, width)
    block_rows = 128
    blocks = entries // block_rows
    owner_ids = jnp.arange(owners_all, dtype=jnp.int32)
    owner_table = (owner.reshape(blocks, block_rows, 1) == owner_ids[None, None, :]).astype(
        jnp.bfloat16
    )
    row_pos = jnp.arange(block_rows, dtype=jnp.int32)
    earlier = (row_pos[:, None] > row_pos[None, :]).astype(jnp.bfloat16)
    within_all = jnp.einsum("ij,bjo->bio", earlier, owner_table, preferred_element_type=jnp.float32)
    block_totals = jnp.sum(owner_table.astype(jnp.float32), axis=1)
    block_start = jnp.cumsum(block_totals, axis=0) - block_totals
    ahead = within_all + block_start[:, None, :]
    rank = jnp.sum(ahead * owner_table.astype(jnp.float32), axis=2).reshape(-1).astype(jnp.int32)
    place = owner * capacity + rank
    send_values = (
        jnp.zeros((owners_all * capacity, width), jnp.bfloat16)
        .at[place]
        .set(values, unique_indices=True)
    )
    send_target = (
        jnp.full((owners_all * capacity,), sentinel, jnp.int32)
        .at[place]
        .set(target, unique_indices=True)
    )
    send_values = send_values.reshape(size_gx, size_gy, capacity, width)
    send_target = send_target.reshape(size_gx, size_gy, capacity)
    got_values, got_target = (
        lax.all_to_all(
            lax.all_to_all(send_values, "gy", split_axis=1, concat_axis=1, tiled=True),
            "gx",
            split_axis=0,
            concat_axis=0,
            tiled=True,
        ),
        lax.all_to_all(
            lax.all_to_all(send_target, "gy", split_axis=1, concat_axis=1, tiled=True),
            "gx",
            split_axis=0,
            concat_axis=0,
            tiled=True,
        ),
    )
    summed = jax.ops.segment_sum(
        got_values.reshape(-1, width).astype(jnp.float32),
        got_target.reshape(-1),
        num_segments=sentinel + 1,
    )
    table_grad = summed[:sentinel].reshape(R_DEV, FIELDS, width)
    return (weight_grad, table_grad)


def solution(mesh):
    placed = (
        P(("gx", "gy"), None, None),
        P(("gx", "gy"), None, None),
        P(),
        P(("gx", "gy"), None, None),
        P(("gx", "gy"), None),
        P(),
    )
    return jax.shard_map(
        on_device,
        mesh=mesh,
        in_specs=placed,
        out_specs=(P(), P(("gx", "gy"), None, None)),
        check_vma=False,
    )
```

profile of v0, /device:TPU:0, one launch (start us, length us, event | category | flops | bytes accessed | tf_op | source)
XLA Modules:
  0.0 339.2 jit_solution(13678758075913814048)
XLA Ops:
  7.2 0.8 fusion.102
  8.0 0.3 copy.219
  8.2 0.3 reshape.231
  8.5 25.5 %gather_fusion = s32[4096]{0:T(1024)S(1)} fusion(s32[8,8192]{1,0:T(8,128)S(1)} %copy-done, s32[4096]{0:T(1024)S(1)} %reshape.231), kind=kCustom, calls=%fused_computation | custom fusion | bytes 65536 | tf_op jit(solution)/shard_map/gather | solution.py:52
  34.0 0.2 convert_reduce_fusion
  34.3 0.3 fusion.4
  34.7 0.2 iota_compare_fusion
  34.9 0.3 lt.51
  35.3 0.3 add.296
  35.7 15.5 %scatter_custom_fusion = s32[8192]{0:T(1024)S(1)} fusion(s32[4096]{0:T(1024)S(1)} %bitcast.64, s32[4096]{0:T(1024)S(1)} %fusion.98, s32[]{:T(128)} %constant.25.clone.1), kind=kCustom, calls=%fused_computation.188 | custom fusion | bytes 32772 | tf_op jit(solution)/shard_map/scatter | solution.py:80
  51.3 0.6 copy.221
  51.9 4.3 %all-to-all-start = ((s32[8,4,256]{2,0,1:T(8,128)}), s32[8,4,256]{2,0,1:T(8,128)S(1)}, u32[]{:S(2)}, u32[]{:S(2)}) async-start(s32[8,4,256]{2,0,1:T(8,128)} %copy.221), calls=%async_computation | async-start | bytes 65536 | tf_op jit(solution)/shard_map/all_to_all | solution.py:93
  56.3 0.4 fusion.109
  56.8 0.1 copy.244
  56.9 0.1 copy.242
  57.1 0.1 copy.240
  57.2 0.1 copy.233
  57.4 0.1 copy.237
  57.6 0.1 copy.239
  57.7 0.1 copy.241
  57.8 0.1 copy.243
  57.9 0.1 copy.245
  58.1 0.1 copy.238
  58.2 0.1 copy.236
  58.3 0.1 copy.234
  58.5 0.1 copy.249
  58.6 0.1 copy.250
  58.7 0.1 copy.251
  58.8 0.1 copy.252
  59.0 0.1 copy.247
  59.1 0.1 copy.248
  59.2 0.1 copy.253
  59.3 0.1 copy.254
  59.5 0.1 copy.255
  59.6 0.1 copy.256
  59.7 0.1 copy.257
  59.8 0.1 copy.258
  60.0 0.1 copy.259
  60.1 0.1 copy.260
  60.2 0.1 copy.261
  60.3 0.1 copy.262
  60.5 0.1 copy.263
  60.6 0.1 copy.264
  60.7 0.1 copy.265
  61.5 0.2 convolution_bitcast_fusion
  61.7 0.4 copy-done.3
  62.2 0.3 convolution_bitcast_fusion.1
  62.9 0.2 copy.226
  63.1 0.4 broadcast_in_dim.61
  63.4 13.8 %scatter_custom_fusion.1 = bf16[8192,128]{1,0:T(8,128)(2,1)S(1)} fusion(s32[4096]{0:T(1024)S(1)} %bitcast.65, bf16[4096,128]{1,0:T(8,128)(2,1)S(1)} %bitcast.58, bf16[]{:T(256)} %constant.49.clone.1, pred[4096]{0:T(1024)(128)(4,1)S(1)} %lt.51), kind=kCustom, calls=%fused_computation.14 | custom fusion | flops 524288 | bytes 3150848 | tf_op jit(solution)/shard_map/scatter | solution.py:75
  77.2 1.5 copy.227
  78.7 3.6 %all-to-all-start.2 = ((bf16[8,4,256,128]{3,2,0,1:T(8,128)(2,1)}), bf16[8,4,256,128]{3,2,0,1:T(8,128)(2,1)S(1)}, u32[]{:S(2)}, u32[]{:S(2)}) async-start(bf16[8,4,256,128]{3,2,0,1:T(8,128)(2,1)} %copy.227), calls=%async_computation.2 | async-start | bytes 4194304 | tf_op jit(solution)/shard_map/all_to_all | solution.py:86
  82.3 0.6 copy.222
  82.9 25.0 %all-to-all-done.2 = bf16[8,4,256,128]{3,2,0,1:T(8,128)(2,1)S(1)} async-done(((bf16[8,4,256,128]{3,2,0,1:T(8,128)(2,1)}), bf16[8,4,256,128]{3,2,0,1:T(8,128)(2,1)S(1)}, u32[]{:S(2)}, u32[]{:S(2)}) %all-to-all-start.2) | async-done | bytes 2097184 | tf_op jit(solution)/shard_map/all_to_all | solution.py:86
  107.9 6.3 %all-to-all-start.1 = ((s32[8,4,256]{2,1,0:T(4,128)}), s32[8,4,256]{2,1,0:T(4,128)S(1)}, u32[]{:S(2)}, u32[]{:S(2)}) async-start(s32[8,4,256]{2,1,0:T(4,128)} %copy.222), calls=%async_computation.1 | async-start | bytes 65536 | tf_op jit(solution)/shard_map/all_to_all | solution.py:92
  114.2 1.5 copy.228
  115.7 5.2 %all-to-all-done.1 = s32[8,4,256]{2,1,0:T(4,128)S(1)} async-done(((s32[8,4,256]{2,1,0:T(4,128)}), s32[8,4,256]{2,1,0:T(4,128)S(1)}, u32[]{:S(2)}, u32[]{:S(2)}) %all-to-all-start.1) | async-done | bytes 32800 | tf_op jit(solution)/shard_map/all_to_all | solution.py:92
  120.9 3.6 %all-to-all-start.3 = ((bf16[8,4,256,128]{3,2,1,0:T(8,128)(2,1)}), bf16[8,4,256,128]{3,2,1,0:T(8,128)(2,1)S(1)}, u32[]{:S(2)}, u32[]{:S(2)}) async-start(bf16[8,4,256,128]{3,2,1,0:T(8,128)(2,1)} %copy.228), calls=%async_computation.3 | async-start | bytes 4194304 | tf_op jit(solution)/shard_map/all_to_all | solution.py:85
  124.5 0.2 all-reduce.2.cloned.1.call-start
  124.8 1.0 convolution_bitcast_fusion.2
  125.8 147.7 %all-reduce.2.cloned.1.call-done = f32[7,128,128]{1,2,0:T(8,128)} async-done(((f32[7,128,128]{1,2,0:T(8,128)}), f32[7,128,128]{1,2,0:T(8,128)}) %all-reduce.2.cloned.1.call-update) | async-done | bytes 458768 | tf_op jit(solution)/shard_map/psum | solution.py:35
  273.5 2.0 copy.229
  275.5 55.8 %scatter_custom_fusion.2 = f32[2049,128]{1,0:T(8,128)S(1)} fusion(s32[8192]{0:T(1024)S(1)} %bitcast.63, bf16[8192,128]{1,0:T(8,128)(2,1)S(1)} %bitcast.56, f32[]{:T(128)} %constant.21.clone.1), kind=kCustom, calls=%fused_computation.4 | custom fusion | flops 2097152 | bytes 3146244 | tf_op jit(solution)/shard_map/scatter-add | solution.py:100
  331.3 1.0 slice_bitcast_fusion
  (49 shorter events, 1.7 us)
Async XLA Ops:
  7.2 1.3 copy-start
  8.5 26.1 %copy-start.7 = (s32[128,8]{0,1:T(8,128)S(1)}, s32[128,8]{0,1:T(8,128)}, u32[]{:S(2)}) copy-start(s32[128,8]{0,1:T(8,128)} %param.10) | copy-start | bytes 12292
  34.0 22.2 %copy-start.6 = (bf16[128,28,128]{2,0,1:T(8,128)(2,1)S(1)}, bf16[128,28,128]{2,0,1:T(8,128)(2,1)}, u32[]{:S(2)}) copy-start(bf16[128,28,128]{2,0,1:T(8,128)(2,1)} %param.7) | copy-start | bytes 2752516
  34.3 22.0 %copy-start.1 = (bf16[128,8,128]{2,1,0:T(8,128)(2,1)S(1)}, bf16[128,8,128]{2,1,0:T(8,128)(2,1)}, u32[]{:S(2)}) copy-start(bf16[128,8,128]{2,1,0:T(8,128)(2,1)} %param.6) | copy-start | bytes 786436
  51.9 26.8 %all-to-all-start = ((s32[8,4,256]{2,0,1:T(8,128)}), s32[8,4,256]{2,0,1:T(8,128)S(1)}, u32[]{:S(2)}, u32[]{:S(2)}) async-start(s32[8,4,256]{2,0,1:T(8,128)} %copy.221), calls=%async_computation | async-start | bytes 65536 | tf_op jit(solution)/shard_map/all_to_all | solution.py:93
  57.3 4.2 %copy-start.5 = (bf16[7,128,128]{2,1,0:T(8,128)(2,1)S(1)}, bf16[7,128,128]{2,1,0:T(8,128)(2,1)}, u32[]{:S(2)}) copy-start(bf16[7,128,128]{2,1,0:T(8,128)(2,1)} %param.8) | copy-start | bytes 688132
  61.5 0.7 copy-start.3
  78.7 29.2 %all-to-all-start.2 = ((bf16[8,4,256,128]{3,2,0,1:T(8,128)(2,1)}), bf16[8,4,256,128]{3,2,0,1:T(8,128)(2,1)S(1)}, u32[]{:S(2)}, u32[]{:S(2)}) async-start(bf16[8,4,256,128]{3,2,0,1:T(8,128)(2,1)} %copy.227), calls=%async_computation.2 | async-start | bytes 4194304 | tf_op jit(solution)/shard_map/all_to_all | solution.py:86
  107.9 13.0 %all-to-all-start.1 = ((s32[8,4,256]{2,1,0:T(4,128)}), s32[8,4,256]{2,1,0:T(4,128)S(1)}, u32[]{:S(2)}, u32[]{:S(2)}) async-start(s32[8,4,256]{2,1,0:T(4,128)} %copy.222), calls=%async_computation.1 | async-start | bytes 65536 | tf_op jit(solution)/shard_map/all_to_all | solution.py:92
  115.7 9.1 %copy-start.2 = (bf16[128,8,128]{2,1,0:T(8,128)(2,1)S(1)}, bf16[128,8,128]{2,1,0:T(8,128)(2,1)}, u32[]{:S(2)}) copy-start(bf16[128,8,128]{2,1,0:T(8,128)(2,1)} %param.6) | copy-start | bytes 786436
  115.7 9.1 %copy-start.4 = (bf16[128,7,128]{0,2,1:T(8,128)(2,1)S(1)}, bf16[128,7,128]{0,2,1:T(8,128)(2,1)}, u32[]{:S(2)}) copy-start(bf16[128,7,128]{0,2,1:T(8,128)(2,1)} %copy-done.3) | copy-start | bytes 688132
  120.9 154.6 %all-to-all-start.3 = ((bf16[8,4,256,128]{3,2,1,0:T(8,128)(2,1)}), bf16[8,4,256,128]{3,2,1,0:T(8,128)(2,1)S(1)}, u32[]{:S(2)}, u32[]{:S(2)}) async-start(bf16[8,4,256,128]{3,2,1,0:T(8,128)(2,1)} %copy.228), calls=%async_computation.3 | async-start | bytes 4194304 | tf_op jit(solution)/shard_map/all_to_all | solution.py:85
  124.5 149.0 %all-reduce.2.cloned.1.call-start = ((), (), s32[]{:S(2)}) async-start(), calls=%async_computation.4 | async-start | bytes 917504 | tf_op jit(solution)/shard_map/psum | solution.py:35
Sparse Core Ops, SparseCore 0:
  131.2 142.2 all-reduce.1
where the time goes:
time: 340 us; the launch traced here: 339 us
  waiting for transfers between devices  178 us (52%)
  other arithmetic  71.7 us (21%)
  local copies, waits for them, and re-layouts  55.3 us (16%)
  starting transfers between devices  18 us (5%)
  between operations  14.5 us (4%)
    psum x1, waiting for transfers between devices, on_device(): weight_grad = lax.psum(local_weight, ('gx', 'gy'))  148 us
    scatter-add x1, other arithmetic, on_device(): jax.ops.segment_sum(got_values.reshape(-1, width).astype(jnp.float32), go...  55.8 us
    gather x1, local copies, waits for them, and re-layouts, on_device(): stored = row_home[field_index, bag_ids]  25.5 us
    all_to_all x1, waiting for transfers between devices, on_device(): lax.all_to_all(send_values, 'gy', split_axis=1, concat_axis=1, tiled=True)  25 us
    scatter x1, local copies, waits for them, and re-layouts, on_device(): send_target = jnp.full((owners_all * capacity,), sentinel, jnp.int32).at[...  15.5 us
    scatter x1, other arithmetic, on_device(): send_values = jnp.zeros((owners_all * capacity, width), jnp.bfloat16).at[...  13.8 us
    unnamed x55, local copies, waits for them, and re-layouts  6.81 us
  transfers between devices with their start and end apart: 5, of which 3 were waited for; matrix products, arithmetic and copies ran while one was open for 8% of the time, Pallas kernels for 0%

commit v1 on v0

--- a/solution.py
+++ b/solution.py
@@ -32,7 +32,7 @@
     local_weight = jnp.einsum(
         "bfd,bfe->fde", pooled[:, : FIELDS - 1], upper_bf, preferred_element_type=jnp.float32
     )
-    weight_grad = lax.psum(local_weight, ("gx", "gy"))
+    weight_grad = lax.psum(lax.psum(local_weight, "gy"), "gx")
     back_terms = jnp.einsum("bfe,fde->bfd", upper_bf, bilinear, preferred_element_type=jnp.float32)
     field_list = []
     for i in range(FIELDS):

time: 340 us -> 304 us (0.89)
  waiting for transfers between devices: 178 us -> 142 us
    psum x1 -> x2, waiting for transfers between devices: 148 us -> 112 us  [on_device(): weight_grad = lax.psum(lax.psum(local_weight, 'gy'), 'gx')]
  transfers between devices with their start and end apart: 5 -> 6, of which waited for: 3 -> 4; matrix products, arithmetic and copies ran while one was open for 8% -> 9% of each run, Pallas kernels for 0% -> 0%
where the time goes in v1:
time: 304 us; the launch traced here: 303 us
  waiting for transfers between devices  142 us (47%)
  other arithmetic  71.7 us (24%)
  local copies, waits for them, and re-layouts  55.3 us (18%)
  starting transfers between devices  17.9 us (6%)
  between operations  14.5 us (5%)
    psum x2, waiting for transfers between devices, on_device(): weight_grad = lax.psum(lax.psum(local_weight, 'gy'), 'gx')  112 us
    scatter-add x1, other arithmetic, on_device(): jax.ops.segment_sum(got_values.reshape(-1, width).astype(jnp.float32), go...  55.8 us
    gather x1, local copies, waits for them, and re-layouts, on_device(): stored = row_home[field_index, bag_ids]  25.5 us
    all_to_all x1, waiting for transfers between devices, on_device(): lax.all_to_all(send_values, 'gy', split_axis=1, concat_axis=1, tiled=True)  25 us
    scatter x1, local copies, waits for them, and re-layouts, on_device(): send_target = jnp.full((owners_all * capacity,), sentinel, jnp.int32).at[...  15.5 us
    scatter x1, other arithmetic, on_device(): send_values = jnp.zeros((owners_all * capacity, width), jnp.bfloat16).at[...  13.8 us
    unnamed x55, local copies, waits for them, and re-layouts  6.81 us
    all_to_all x1, starting transfers between devices, on_device(): lax.all_to_all(lax.all_to_all(send_target, 'gy', split_axis=1, concat_axi...  6.3 us
  transfers between devices with their start and end apart: 6, of which 4 were waited for; matrix products, arithmetic and copies ran while one was open for 9% of the time, Pallas kernels for 0%

profile of v1, /device:TPU:0, one launch (start us, length us, event | category | flops | bytes accessed | tf_op | source)
XLA Modules:
  0.0 303.1 jit_solution(15989298663088115606)
XLA Ops:
  7.2 0.8 fusion.102
  8.0 0.3 copy.219
  8.2 0.3 reshape.231
  8.5 25.5 %gather_fusion = s32[4096]{0:T(1024)S(1)} fusion(s32[8,8192]{1,0:T(8,128)S(1)} %copy-done, s32[4096]{0:T(1024)S(1)} %reshape.231), kind=kCustom, calls=%fused_computation | custom fusion | bytes 65536 | tf_op jit(solution)/shard_map/gather | solution.py:52
  34.0 0.2 convert_reduce_fusion
  34.3 0.3 fusion.4
  34.7 0.2 iota_compare_fusion
  34.9 0.3 lt.51
  35.3 0.3 add.298
  35.7 15.5 %scatter_custom_fusion = s32[8192]{0:T(1024)S(1)} fusion(s32[4096]{0:T(1024)S(1)} %bitcast.64, s32[4096]{0:T(1024)S(1)} %fusion.98, s32[]{:T(128)} %constant.25.clone.1), kind=kCustom, calls=%fused_computation.188 | custom fusion | bytes 32772 | tf_op jit(solution)/shard_map/scatter | solution.py:80
  51.3 0.6 copy.221
  51.9 4.3 %all-to-all-start = ((s32[8,4,256]{2,0,1:T(8,128)}), s32[8,4,256]{2,0,1:T(8,128)S(1)}, u32[]{:S(2)}, u32[]{:S(2)}) async-start(s32[8,4,256]{2,0,1:T(8,128)} %copy.221), calls=%async_computation | async-start | bytes 65536 | tf_op jit(solution)/shard_map/all_to_all | solution.py:93
  56.3 0.4 fusion.109
  56.8 0.1 copy.244
  56.9 0.1 copy.242
  57.1 0.1 copy.240
  57.2 0.1 copy.233
  57.4 0.1 copy.237
  57.6 0.1 copy.239
  57.7 0.1 copy.241
  57.8 0.1 copy.243
  57.9 0.1 copy.245
  58.1 0.1 copy.238
  58.2 0.1 copy.236
  58.3 0.1 copy.234
  58.5 0.1 copy.249
  58.6 0.1 copy.250
  58.7 0.1 copy.251
  58.8 0.1 copy.252
  59.0 0.1 copy.247
  59.1 0.1 copy.248
  59.2 0.1 copy.253
  59.3 0.1 copy.254
  59.5 0.1 copy.255
  59.6 0.1 copy.256
  59.7 0.1 copy.257
  59.8 0.1 copy.258
  60.0 0.1 copy.259
  60.1 0.1 copy.260
  60.2 0.1 copy.261
  60.3 0.1 copy.262
  60.5 0.1 copy.263
  60.6 0.1 copy.264
  60.7 0.1 copy.265
  61.5 0.2 convolution_bitcast_fusion
  61.7 0.4 copy-done.3
  62.2 0.3 convolution_bitcast_fusion.1
  62.9 0.2 copy.226
  63.1 0.4 broadcast_in_dim.61
  63.4 13.8 %scatter_custom_fusion.1 = bf16[8192,128]{1,0:T(8,128)(2,1)S(1)} fusion(s32[4096]{0:T(1024)S(1)} %bitcast.65, bf16[4096,128]{1,0:T(8,128)(2,1)S(1)} %bitcast.58, bf16[]{:T(256)} %constant.49.clone.1, pred[4096]{0:T(1024)(128)(4,1)S(1)} %lt.51), kind=kCustom, calls=%fused_computation.14 | custom fusion | flops 524288 | bytes 3150848 | tf_op jit(solution)/shard_map/scatter | solution.py:75
  77.2 1.5 copy.227
  78.7 3.6 %all-to-all-start.2 = ((bf16[8,4,256,128]{3,2,0,1:T(8,128)(2,1)}), bf16[8,4,256,128]{3,2,0,1:T(8,128)(2,1)S(1)}, u32[]{:S(2)}, u32[]{:S(2)}) async-start(bf16[8,4,256,128]{3,2,0,1:T(8,128)(2,1)} %copy.227), calls=%async_computation.2 | async-start | bytes 4194304 | tf_op jit(solution)/shard_map/all_to_all | solution.py:86
  82.3 0.6 copy.222
  82.9 25.0 %all-to-all-done.2 = bf16[8,4,256,128]{3,2,0,1:T(8,128)(2,1)S(1)} async-done(((bf16[8,4,256,128]{3,2,0,1:T(8,128)(2,1)}), bf16[8,4,256,128]{3,2,0,1:T(8,128)(2,1)S(1)}, u32[]{:S(2)}, u32[]{:S(2)}) %all-to-all-start.2) | async-done | bytes 2097184 | tf_op jit(solution)/shard_map/all_to_all | solution.py:86
  107.9 6.3 %all-to-all-start.1 = ((s32[8,4,256]{2,1,0:T(4,128)}), s32[8,4,256]{2,1,0:T(4,128)S(1)}, u32[]{:S(2)}, u32[]{:S(2)}) async-start(s32[8,4,256]{2,1,0:T(4,128)} %copy.222), calls=%async_computation.1 | async-start | bytes 65536 | tf_op jit(solution)/shard_map/all_to_all | solution.py:92
  114.2 1.5 copy.228
  115.7 5.2 %all-to-all-done.1 = s32[8,4,256]{2,1,0:T(4,128)S(1)} async-done(((s32[8,4,256]{2,1,0:T(4,128)}), s32[8,4,256]{2,1,0:T(4,128)S(1)}, u32[]{:S(2)}, u32[]{:S(2)}) %all-to-all-start.1) | async-done | bytes 32800 | tf_op jit(solution)/shard_map/all_to_all | solution.py:92
  120.9 3.6 %all-to-all-start.3 = ((bf16[8,4,256,128]{3,2,1,0:T(8,128)(2,1)}), bf16[8,4,256,128]{3,2,1,0:T(8,128)(2,1)S(1)}, u32[]{:S(2)}, u32[]{:S(2)}) async-start(bf16[8,4,256,128]{3,2,1,0:T(8,128)(2,1)} %copy.228), calls=%async_computation.3 | async-start | bytes 4194304 | tf_op jit(solution)/shard_map/all_to_all | solution.py:85
  124.6 1.0 convolution_bitcast_fusion.2
  125.6 36.1 %all-reduce.3.cloned.1.call-done = f32[7,128,128]{1,2,0:T(8,128)} async-done(((f32[7,128,128]{1,2,0:T(8,128)}), f32[7,128,128]{1,2,0:T(8,128)}) %all-reduce.3.cloned.1.call-update) | async-done | bytes 458768 | tf_op jit(solution)/shard_map/psum | solution.py:35
  161.8 75.6 %all-reduce.5.cloned.1.call-done = f32[7,128,128]{1,2,0:T(8,128)} async-done(((f32[7,128,128]{1,2,0:T(8,128)}), f32[7,128,128]{1,2,0:T(8,128)}) %all-reduce.5.cloned.1.call-update) | async-done | bytes 458768 | tf_op jit(solution)/shard_map/psum | solution.py:35
  237.4 2.0 copy.229
  239.4 55.8 %scatter_custom_fusion.2 = f32[2049,128]{1,0:T(8,128)S(1)} fusion(s32[8192]{0:T(1024)S(1)} %bitcast.63, bf16[8192,128]{1,0:T(8,128)(2,1)S(1)} %bitcast.56, f32[]{:T(128)} %constant.21.clone.1), kind=kCustom, calls=%fused_computation.4 | custom fusion | flops 2097152 | bytes 3146244 | tf_op jit(solution)/shard_map/scatter-add | solution.py:100
  295.2 1.0 slice_bitcast_fusion
  (52 shorter events, 1.8 us)
Async XLA Ops:
  7.2 1.3 copy-start
  8.5 26.1 %copy-start.7 = (s32[128,8]{0,1:T(8,128)S(1)}, s32[128,8]{0,1:T(8,128)}, u32[]{:S(2)}) copy-start(s32[128,8]{0,1:T(8,128)} %param.10) | copy-start | bytes 12292
  34.0 22.2 %copy-start.6 = (bf16[128,28,128]{2,0,1:T(8,128)(2,1)S(1)}, bf16[128,28,128]{2,0,1:T(8,128)(2,1)}, u32[]{:S(2)}) copy-start(bf16[128,28,128]{2,0,1:T(8,128)(2,1)} %param.7) | copy-start | bytes 2752516
  34.3 22.0 %copy-start.1 = (bf16[128,8,128]{2,1,0:T(8,128)(2,1)S(1)}, bf16[128,8,128]{2,1,0:T(8,128)(2,1)}, u32[]{:S(2)}) copy-start(bf16[128,8,128]{2,1,0:T(8,128)(2,1)} %param.6) | copy-start | bytes 786436
  51.9 26.8 %all-to-all-start = ((s32[8,4,256]{2,0,1:T(8,128)}), s32[8,4,256]{2,0,1:T(8,128)S(1)}, u32[]{:S(2)}, u32[]{:S(2)}) async-start(s32[8,4,256]{2,0,1:T(8,128)} %copy.221), calls=%async_computation | async-start | bytes 65536 | tf_op jit(solution)/shard_map/all_to_all | solution.py:93
  57.3 4.2 %copy-start.5 = (bf16[7,128,128]{2,1,0:T(8,128)(2,1)S(1)}, bf16[7,128,128]{2,1,0:T(8,128)(2,1)}, u32[]{:S(2)}) copy-start(bf16[7,128,128]{2,1,0:T(8,128)(2,1)} %param.8) | copy-start | bytes 688132
  61.5 0.7 copy-start.3
  78.7 29.3 %all-to-all-start.2 = ((bf16[8,4,256,128]{3,2,0,1:T(8,128)(2,1)}), bf16[8,4,256,128]{3,2,0,1:T(8,128)(2,1)S(1)}, u32[]{:S(2)}, u32[]{:S(2)}) async-start(bf16[8,4,256,128]{3,2,0,1:T(8,128)(2,1)} %copy.227), calls=%async_computation.2 | async-start | bytes 4194304 | tf_op jit(solution)/shard_map/all_to_all | solution.py:86
  107.9 13.0 %all-to-all-start.1 = ((s32[8,4,256]{2,1,0:T(4,128)}), s32[8,4,256]{2,1,0:T(4,128)S(1)}, u32[]{:S(2)}, u32[]{:S(2)}) async-start(s32[8,4,256]{2,1,0:T(4,128)} %copy.222), calls=%async_computation.1 | async-start | bytes 65536 | tf_op jit(solution)/shard_map/all_to_all | solution.py:92
  115.7 8.9 %copy-start.2 = (bf16[128,8,128]{2,1,0:T(8,128)(2,1)S(1)}, bf16[128,8,128]{2,1,0:T(8,128)(2,1)}, u32[]{:S(2)}) copy-start(bf16[128,8,128]{2,1,0:T(8,128)(2,1)} %param.6) | copy-start | bytes 786436
  115.7 8.9 %copy-start.4 = (bf16[128,7,128]{0,2,1:T(8,128)(2,1)S(1)}, bf16[128,7,128]{0,2,1:T(8,128)(2,1)}, u32[]{:S(2)}) copy-start(bf16[128,7,128]{0,2,1:T(8,128)(2,1)} %copy-done.3) | copy-start | bytes 688132
  120.9 118.5 %all-to-all-start.3 = ((bf16[8,4,256,128]{3,2,1,0:T(8,128)(2,1)}), bf16[8,4,256,128]{3,2,1,0:T(8,128)(2,1)S(1)}, u32[]{:S(2)}, u32[]{:S(2)}) async-start(bf16[8,4,256,128]{3,2,1,0:T(8,128)(2,1)} %copy.228), calls=%async_computation.3 | async-start | bytes 4194304 | tf_op jit(solution)/shard_map/all_to_all | solution.py:85
  124.5 37.2 %all-reduce.3.cloned.1.call-start = ((), (), s32[]{:S(2)}) async-start(), calls=%async_computation.4 | async-start | bytes 917504 | tf_op jit(solution)/shard_map/psum | solution.py:35
  125.6 111.9 %all-reduce.5.cloned.1.call-start = ((), (), s32[]{:S(2)}) async-start(), calls=%async_computation.5 | async-start | bytes 917504 | tf_op jit(solution)/shard_map/psum | solution.py:35
Sparse Core Ops, SparseCore 0:
  128.3 33.4 all-reduce.2
  165.2 72.2 all-reduce.4
